TPU v7x, 32 devices: a whole 2x2x4 slice. The times are simulated.
32 devices in a mesh: fsdp: 2 (over x), ctx: 4 (over y, core), tp: 4 (over z).
Axes of the slice: x: 2, y: 2, z: 4, core: 2. Of those that a mesh axis runs over, the one named last changes fastest.
Arguments:
- hidden_in: bfloat16 [32, 512, 768], P('fsdp', 'ctx'), may hold values from -6 to 6
- lengths: int32 [32], P('fsdp'), may hold values from 128 to 512, as said below
- cotangent: bfloat16 [32, 512, 768], P('fsdp', 'ctx'), may hold values from -6 to 6
- w_qkv: bfloat16 [768, 3, 768], P(('fsdp', 'ctx'), None, 'tp'), may hold values from -0.21875 to 0.21875
- b_qv: bfloat16 [2, 768], P(None, 'tp'), may hold values from -1.5 to 1.5
- w_out: bfloat16 [768, 768], P('tp', ('fsdp', 'ctx')), may hold values from -2.5 to 2.5
- b_out: bfloat16 [768], P(('fsdp', 'ctx')), may hold values from -1.5 to 1.5
- gain_one: bfloat16 [768], P(('fsdp', 'ctx')), may hold values from 0.5 to 1.5
- shift_one: bfloat16 [768], P(('fsdp', 'ctx')), may hold values from -1.5 to 1.5
- w_in: bfloat16 [768, 3072], P(('fsdp', 'ctx'), 'tp'), may hold values from -0.21875 to 0.21875
- b_in: bfloat16 [3072], P('tp'), may hold values from -1.5 to 1.5
- w_down: bfloat16 [3072, 768], P('tp', ('fsdp', 'ctx')), may hold values from -0.109375 to 0.109375
- b_down: bfloat16 [768], P(('fsdp', 'ctx')), may hold values from -1.5 to 1.5
- gain_two: bfloat16 [768], P(('fsdp', 'ctx')), may hold values from 0.5 to 1.5
- shift_two: bfloat16 [768], P(('fsdp', 'ctx')), may hold values from -1.5 to 1.5
Outputs:
- hidden_out: bfloat16 [32, 512, 768], P('fsdp', 'ctx')
- grad_in: bfloat16 [32, 512, 768], P('fsdp', 'ctx')
- grad_w_qkv: float32 [768, 3, 768], P(('fsdp', 'ctx'), None, 'tp')
- grad_b_qv: float32 [2, 768], P(None, 'tp')
- grad_w_out: float32 [768, 768], P('tp', ('fsdp', 'ctx'))
- grad_b_out: float32 [768], P(('fsdp', 'ctx'))
- grad_gain_one: float32 [768], P(('fsdp', 'ctx'))
- grad_shift_one: float32 [768], P(('fsdp', 'ctx'))
- grad_w_in: float32 [768, 3072], P(('fsdp', 'ctx'), 'tp')
- grad_b_in: float32 [3072], P('tp')
- grad_w_down: float32 [3072, 768], P('tp', ('fsdp', 'ctx'))
- grad_b_down: float32 [768], P(('fsdp', 'ctx'))
- grad_gain_two: float32 [768], P(('fsdp', 'ctx'))
- grad_shift_two: float32 [768], P(('fsdp', 'ctx'))
Inputs may be any that keep to these rules, and one draw needn't show every extreme that they name: The first lengths[s] positions of slot s are valid, the rest padding; some slot has 512 and some 512 // 4.
All inputs are finite; a program needn't handle non-finite values.
Results may differ from a plain program's by a relative error of at most 0.015.
The roundings to bfloat16 on the way count: a program that leaves them out, or rounds other values in their place, can miss the bound.
Values may be sent and summed in bfloat16 or wider, within the bound.
A program may use at most 192 MiB of HBM per device.

v0:
```python
import jax
import jax.numpy as jnp
from jax import lax
from jax.sharding import PartitionSpec as P

HD = 64
SLOT_MB = 4
epsilon = 1e-05


def tp_total(partial_sum):
    return lax.psum(partial_sum, "tp")


def layer_norm(summed, gain_row, shift_row):
    center = summed - jnp.mean(summed, axis=-1, keepdims=True)
    inverse = lax.rsqrt(jnp.mean(center * center, axis=-1, keepdims=True) + epsilon)
    normed = center * inverse
    return (normed * gain_row + shift_row, normed, inverse)


def norm_back(incoming, normed, inverse, gain_row):
    scaled = incoming * gain_row
    result = inverse * (
        scaled
        - jnp.mean(scaled, axis=-1, keepdims=True)
        - normed * jnp.mean(scaled * normed, axis=-1, keepdims=True)
    )
    return (result, jnp.sum(incoming * normed, axis=0), jnp.sum(incoming, axis=0))


def attn_scores(queries, keys_all, key_valid, score_scale):
    raw_scores = (
        jnp.einsum("bqhe,bkhe->bhqk", queries, keys_all, preferred_element_type=jnp.float32)
        * score_scale
    )
    return jnp.where(key_valid[:, None, None, :], raw_scores, -1e30)


def on_device(
    hidden_in,
    lengths,
    cotangent,
    w_qkv,
    b_qv,
    w_out,
    b_out,
    gain_one,
    shift_one,
    w_in,
    b_in,
    w_down,
    b_down,
    gain_two,
    shift_two,
):
    local_slots, row_count, model_width = hidden_in.shape
    slot_batch = SLOT_MB
    micro_count = local_slots // slot_batch
    flat_rows = slot_batch * row_count
    key_count = row_count * lax.axis_size("ctx")
    local_width = w_qkv.shape[2]
    head_count = local_width // HD
    score_scale = HD ** (-0.5)
    row_place = lax.axis_index("ctx") * row_count + jnp.arange(row_count, dtype=jnp.int32)
    key_place = jnp.arange(key_count, dtype=jnp.int32)
    bias_three = jnp.stack([b_qv[0], jnp.zeros_like(b_qv[0]), b_qv[1]]).astype(jnp.float32)
    bias_in = b_in.astype(jnp.float32)
    bias_grads = (jnp.zeros((2, local_width), jnp.float32), jnp.zeros(b_in.shape, jnp.float32))
    outputs = []
    input_grads = []
    for micro_index in range(micro_count):
        gathered = (
            lax.all_gather(w_qkv, ("fsdp", "ctx"), axis=0, tiled=True),
            lax.all_gather(w_out, ("fsdp", "ctx"), axis=1, tiled=True),
            lax.all_gather(w_in, ("fsdp", "ctx"), axis=0, tiled=True),
            lax.all_gather(w_down, ("fsdp", "ctx"), axis=1, tiled=True),
            lax.all_gather(b_out, ("fsdp", "ctx"), axis=0, tiled=True),
            lax.all_gather(gain_one, ("fsdp", "ctx"), axis=0, tiled=True),
            lax.all_gather(shift_one, ("fsdp", "ctx"), axis=0, tiled=True),
            lax.all_gather(b_down, ("fsdp", "ctx"), axis=0, tiled=True),
            lax.all_gather(gain_two, ("fsdp", "ctx"), axis=0, tiled=True),
            lax.all_gather(shift_two, ("fsdp", "ctx"), axis=0, tiled=True),
        )
        full_qkv, full_out, full_in, full_down = (
            gathered[0],
            gathered[1],
            gathered[2],
            gathered[3],
        )
        full_bout = gathered[4].astype(jnp.float32)
        full_gain_one = gathered[5].astype(jnp.float32)
        full_shift_one = gathered[6].astype(jnp.float32)
        full_bdown = gathered[7].astype(jnp.float32)
        full_gain_two = gathered[8].astype(jnp.float32)
        full_shift_two = gathered[9].astype(jnp.float32)
        first_slot = micro_index * slot_batch
        tokens = hidden_in[first_slot : first_slot + slot_batch].reshape(flat_rows, model_width)
        length = lengths[first_slot : first_slot + slot_batch]
        row_valid = (row_place[None, :] < length[:, None]).astype(jnp.float32).reshape(flat_rows)
        key_valid = key_place[None, :] < length[:, None]
        qkv_local = (
            jnp.einsum("sd,dcf->scf", tokens, full_qkv, preferred_element_type=jnp.float32)
            + bias_three
        ).astype(jnp.bfloat16)
        kv_local = qkv_local[:, 1:].reshape(slot_batch, row_count, 2, local_width)
        key_value = lax.all_gather(kv_local, "ctx", axis=1, tiled=True)
        queries = qkv_local[:, 0].reshape(slot_batch, row_count, head_count, HD)
        keys_all = key_value[:, :, 0].reshape(slot_batch, key_count, head_count, HD)
        values_all = key_value[:, :, 1].reshape(slot_batch, key_count, head_count, HD)
        scores = attn_scores(queries, keys_all, key_valid, score_scale)
        highest = jnp.max(scores, axis=-1, keepdims=True)
        exponent = jnp.exp(scores - highest)
        denominator = jnp.sum(exponent, axis=-1, keepdims=True)
        log_total = highest + jnp.log(denominator)
        probs_low = (exponent / denominator).astype(jnp.bfloat16)
        context = (
            jnp.einsum("bhqk,bkhe->bqhe", probs_low, values_all, preferred_element_type=jnp.float32)
            .astype(jnp.bfloat16)
            .reshape(flat_rows, local_width)
        )
        attended = (
            tp_total(jnp.dot(context, full_out, preferred_element_type=jnp.float32)) + full_bout
        )
        first_out, normed_one, inverse_one = layer_norm(
            tokens.astype(jnp.float32) + attended, full_gain_one, full_shift_one
        )
        first_low = first_out.astype(jnp.bfloat16)
        pre_act = jnp.dot(first_low, full_in, preferred_element_type=jnp.float32) + bias_in
        activated = jax.nn.gelu(pre_act, approximate=False).astype(jnp.bfloat16)
        branch = (
            tp_total(jnp.dot(activated, full_down, preferred_element_type=jnp.float32)) + full_bdown
        )
        result, normed_two, inverse_two = layer_norm(
            first_out + branch, full_gain_two, full_shift_two
        )
        outputs.append(result.astype(jnp.bfloat16).reshape(slot_batch, row_count, model_width))
        incoming = (
            cotangent[first_slot : first_slot + slot_batch]
            .reshape(flat_rows, model_width)
            .astype(jnp.float32)
            * row_valid[:, None]
        )
        grad_two, grad_gain_two, grad_shift_two = norm_back(
            incoming, normed_two, inverse_two, full_gain_two
        )
        grad_branch = grad_two.astype(jnp.bfloat16)
        grad_bdown = jnp.sum(grad_branch.astype(jnp.float32), axis=0)
        grad_wdown = jnp.einsum(
            "sf,sd->fd", activated, grad_branch, preferred_element_type=jnp.float32
        )
        grad_act = jnp.einsum(
            "sd,fd->sf", grad_branch, full_down, preferred_element_type=jnp.float32
        )
        _, gelu_back = jax.vjp(
            lambda inner_value: jax.nn.gelu(inner_value, approximate=False), pre_act
        )
        grad_pre = gelu_back(grad_act)[0].astype(jnp.bfloat16)
        grad_win = jnp.einsum("sd,sf->df", first_low, grad_pre, preferred_element_type=jnp.float32)
        grad_bin = jnp.sum(grad_pre.astype(jnp.float32), axis=0)
        grad_first = grad_two + tp_total(
            jnp.einsum("sf,df->sd", grad_pre, full_in, preferred_element_type=jnp.float32)
        )
        grad_one, grad_gain_one, grad_shift_one = norm_back(
            grad_first, normed_one, inverse_one, full_gain_one
        )
        grad_attended = grad_one.astype(jnp.bfloat16)
        grad_bout = jnp.sum(grad_attended.astype(jnp.float32), axis=0)
        grad_wout = jnp.einsum(
            "sf,sd->fd", context, grad_attended, preferred_element_type=jnp.float32
        )
        grad_context = (
            jnp.einsum("sd,fd->sf", grad_attended, full_out, preferred_element_type=jnp.float32)
            .astype(jnp.bfloat16)
            .reshape(slot_batch, row_count, head_count, HD)
        )
        scores_again = attn_scores(queries, keys_all, key_valid, score_scale)
        weights_back = jnp.exp(scores_again - log_total)
        grad_probs = jnp.einsum(
            "bqhe,bkhe->bhqk", grad_context, values_all, preferred_element_type=jnp.float32
        )
        grad_scores = (
            weights_back * (grad_probs - jnp.sum(grad_probs * weights_back, axis=-1, keepdims=True))
        ).astype(jnp.bfloat16)
        grad_query = (
            jnp.einsum("bhqk,bkhe->bqhe", grad_scores, keys_all, preferred_element_type=jnp.float32)
            * score_scale
        )
        grad_key = (
            jnp.einsum("bhqk,bqhe->bkhe", grad_scores, queries, preferred_element_type=jnp.float32)
            * score_scale
        )
        grad_value = jnp.einsum(
            "bhqk,bqhe->bkhe",
            weights_back.astype(jnp.bfloat16),
            grad_context,
            preferred_element_type=jnp.float32,
        )
        key_value_terms = jnp.stack(
            [
                grad_key.reshape(slot_batch, key_count, local_width),
                grad_value.reshape(slot_batch, key_count, local_width),
            ],
            axis=2,
        )
        key_value_grad = lax.psum_scatter(key_value_terms, "ctx", scatter_dimension=1, tiled=True)
        grad_qkv = (
            jnp.concatenate(
                [grad_query.reshape(slot_batch, row_count, 1, local_width), key_value_grad], axis=2
            )
            .astype(jnp.bfloat16)
            .reshape(flat_rows, 3, local_width)
        )
        grad_wqkv = jnp.einsum("sd,scf->dcf", tokens, grad_qkv, preferred_element_type=jnp.float32)
        qkv_sums = jnp.sum(grad_qkv.astype(jnp.float32), axis=0)
        grad_bqv = jnp.stack([qkv_sums[0], qkv_sums[2]])
        grad_tokens = grad_one + tp_total(
            jnp.einsum("scf,dcf->sd", grad_qkv, full_qkv, preferred_element_type=jnp.float32)
        )
        input_grads.append(
            grad_tokens.astype(jnp.bfloat16).reshape(slot_batch, row_count, model_width)
        )
        bias_grads = (bias_grads[0] + grad_bqv, bias_grads[1] + grad_bin)
        pieces = (
            lax.psum_scatter(grad_wqkv, ("fsdp", "ctx"), scatter_dimension=0, tiled=True),
            lax.psum_scatter(grad_wout, ("fsdp", "ctx"), scatter_dimension=1, tiled=True),
            lax.psum_scatter(grad_win, ("fsdp", "ctx"), scatter_dimension=0, tiled=True),
            lax.psum_scatter(grad_wdown, ("fsdp", "ctx"), scatter_dimension=1, tiled=True),
            lax.psum_scatter(grad_bout, ("fsdp", "ctx"), scatter_dimension=0, tiled=True),
            lax.psum_scatter(grad_gain_one, ("fsdp", "ctx"), scatter_dimension=0, tiled=True),
            lax.psum_scatter(grad_shift_one, ("fsdp", "ctx"), scatter_dimension=0, tiled=True),
            lax.psum_scatter(grad_bdown, ("fsdp", "ctx"), scatter_dimension=0, tiled=True),
            lax.psum_scatter(grad_gain_two, ("fsdp", "ctx"), scatter_dimension=0, tiled=True),
            lax.psum_scatter(grad_shift_two, ("fsdp", "ctx"), scatter_dimension=0, tiled=True),
        )
        grad_shards = pieces if micro_index == 0 else jax.tree.map(jnp.add, grad_shards, pieces)
    bias_total = lax.psum((bias_grads[0], bias_grads[1]), ("fsdp", "ctx"))
    return (
        jnp.concatenate(outputs, axis=0),
        jnp.concatenate(input_grads, axis=0),
        grad_shards[0],
        bias_total[0],
        grad_shards[1],
        grad_shards[4],
        grad_shards[5],
        grad_shards[6],
        grad_shards[2],
        bias_total[1],
        grad_shards[3],
        grad_shards[7],
        grad_shards[8],
        grad_shards[9],
    )


def solution(mesh):
    return jax.shard_map(
        on_device,
        mesh=mesh,
        in_specs=(
            P("fsdp", "ctx", None),
            P("fsdp"),
            P("fsdp", "ctx", None),
            P(("fsdp", "ctx"), None, "tp"),
            P(None, "tp"),
            P("tp", ("fsdp", "ctx")),
            P(("fsdp", "ctx")),
            P(("fsdp", "ctx")),
            P(("fsdp", "ctx")),
            P(("fsdp", "ctx"), "tp"),
            P("tp"),
            P("tp", ("fsdp", "ctx")),
            P(("fsdp", "ctx")),
            P(("fsdp", "ctx")),
            P(("fsdp", "ctx")),
        ),
        out_specs=(
            P("fsdp", "ctx", None),
            P("fsdp", "ctx", None),
            P(("fsdp", "ctx"), None, "tp"),
            P(None, "tp"),
            P("tp", ("fsdp", "ctx")),
            P(("fsdp", "ctx")),
            P(("fsdp", "ctx")),
            P(("fsdp", "ctx")),
            P(("fsdp", "ctx"), "tp"),
            P("tp"),
            P("tp", ("fsdp", "ctx")),
            P(("fsdp", "ctx")),
            P(("fsdp", "ctx")),
            P(("fsdp", "ctx")),
        ),
        check_vma=False,
    )
```

profile of v0, /device:TPU:0, one launch (start us, length us, event | category | flops | bytes accessed | tf_op | source)
XLA Modules:
  0.0 1470.3 jit_solution(5045254554735531446)
XLA Ops:
  8.1 3.0 fusion.200
  11.2 15.5 %all_gather.28 = bf16[768,3,192]{2,1,0:T(4,128)(2,1)} all-gather(bf16[96,3,192]{2,1,0:T(4,128)(2,1)S(1)} %copy.105), channel_id=1, replica_groups=mesh['fsdp'=2,'ctx'=4,'tp'=4] {'fsdp','ctx'}, dimensions={0}, use_global_device_ids=true | all-gather | bytes 995328 | tf_op jit(solution)/shard_map/all_gather | solution.py:74
  26.7 2.6 copy.106
  38.8 9.6 all_gather.30
  51.6 4.2 all-gather.17.cloned.1.call-done
  58.0 19.4 %all-gather.15.cloned.1.call-done = bf16[4,512,2,192]{1,0,3,2:T(4,128)(2,1)} async-done(((bf16[4,128,2,192]{1,0,3,2:T(4,128)(2,1)}), bf16[4,512,2,192]{1,0,3,2:T(4,128)(2,1)}) %all-gather.15.cloned.1.call-update) | async-done | bytes 1572880 | tf_op jit(solution)/shard_map/all_gather | solution.py:107
  88.4 10.5 all-gather.13.cloned.1.call-done
  110.2 9.9 all-gather.7.cloned.1.call-done
  136.2 25.5 %all-reduce.17 = (bf16[768]{0:T(1024)(128)(2,1)}, bf16[768]{0:T(1024)(128)(2,1)}, bf16[768]{0:T(1024)(128)(2,1)}, bf16[768]{0:T(1024)(128)(2,1)}, bf16[768]{0:T(1024)(128)(2,1)}, /*index=5*/bf16[768]{0:T(1024)(128)(2,1)}) all-reduce(bf16[768]{0:T(1024)(128)(2,1)S(1)} %dynamic-update-slice, ...), channel_id=1, replica_groups=mesh['fsdp'=2,'ctx'=4,'tp'=4] {'fsdp','ctx'}, use_global_device_ids=true, to_apply=%add | all-reduce | flops 4608 | bytes 18432
  163.7 187.5 %all-reduce.29.cloned.1.call-done = (f32[512,768]{1,0:T(8,128)}, f32[512,768]{1,0:T(8,128)}, f32[512,768]{1,0:T(8,128)}, f32[512,768]{1,0:T(8,128)}) async-done(((f32[512,768]{1,0:T(8,128)}, f32[512,768]{1,0:T(8,128)}, f32[512,768]{1,0:T(8,128)}, f32[512,768]{1,0:T(8,128)}), (f32[512,768]{1,0:T(8,128)}, f32[512,768]{1,0:T(8,128)}, f32[512,768]{1,0:T(8,128)}, ...) | async-done | bytes 6291472 | tf_op jit(solution)/shard_map/psum | solution.py:12
  351.3 4.6 fusion.193
  360.4 7.9 multiply_convert_fusion.4
  368.3 5.7 multiply_convert_fusion.5
  374.0 3.6 fusion.223
  377.6 2.0 fusion.221
  379.6 5.5 multiply_convert_fusion.6
  385.1 2.0 fusion.219
  387.1 5.8 multiply_convert_fusion.7
  393.8 2.0 fusion.217
  400.3 3.8 multiply_reduce_fusion.23
  405.3 212.5 %all-reduce.27.cloned.1.call-done = (f32[512,768]{1,0:T(8,128)}, f32[512,768]{1,0:T(8,128)}, f32[512,768]{1,0:T(8,128)}, f32[512,768]{1,0:T(8,128)}) async-done(((f32[512,768]{1,0:T(8,128)}, f32[512,768]{1,0:T(8,128)}, f32[512,768]{1,0:T(8,128)}, f32[512,768]{1,0:T(8,128)}), (f32[512,768]{1,0:T(8,128)}, f32[512,768]{1,0:T(8,128)}, f32[512,768]{1,0:T(8,128)}, ...) | async-done | bytes 6291472 | tf_op jit(solution)/shard_map/psum | solution.py:12
  617.8 2.6 fusion.191
  622.0 3.1 fusion.188
  627.0 2.7 multiply_reduce_fusion.4
  631.7 3.1 convert_reduce_fusion.2
  634.8 3.1 convert_reduce_fusion.3
  640.5 2.1 fusion.227
  645.0 2.0 fusion.226
  649.6 2.0 fusion.225
  654.9 2.0 fusion.224
  657.7 221.2 %all-reduce.25.cloned.1.call-done = (f32[512,768]{1,0:T(8,128)}, f32[512,768]{1,0:T(8,128)}, f32[512,768]{1,0:T(8,128)}, f32[512,768]{1,0:T(8,128)}) async-done(((f32[512,768]{1,0:T(8,128)}, f32[512,768]{1,0:T(8,128)}, f32[512,768]{1,0:T(8,128)}, f32[512,768]{1,0:T(8,128)}), (f32[512,768]{1,0:T(8,128)}, f32[512,768]{1,0:T(8,128)}, f32[512,768]{1,0:T(8,128)}, ...) | async-done | bytes 6291472 | tf_op jit(solution)/shard_map/psum | solution.py:12
  879.0 5.5 multiply_reduce_fusion.11
  885.9 3.8 convert_reduce_fusion.11
  889.7 3.8 convert_reduce_fusion.10
  897.5 3.4 multiply_reduce_fusion.1
  903.7 2.0 pad_maximum_fusion.3
  906.5 2.5 convolution_convert_fusion.2
  910.6 4.0 multiply_reduce_fusion.2
  917.6 1.9 pad_maximum_fusion.2
  920.3 2.5 convolution_convert_fusion.3
  924.5 2.3 multiply_reduce_fusion.3
  929.6 1.9 pad_maximum_fusion.1
  932.7 2.5 convolution_convert_fusion
  936.2 2.2 multiply_reduce_fusion
  941.2 2.0 pad_maximum_fusion.4
  957.7 2.8 fusion.73
  960.5 22.3 %reduce-scatter.15.cloned.1.call-done = f32[4,128,2,192]{1,3,0,2:T(8,128)} async-done(((f32[4,512,2,192]{1,3,0,2:T(8,128)}), f32[4,128,2,192]{1,3,0,2:T(8,128)}) %reduce-scatter.15.cloned.1.call-update) | async-done | bytes 786448 | tf_op jit(solution)/shard_map/reduce_scatter | solution.py:206
  982.8 2.0 convert.55
  984.8 38.1 %reduce-scatter.13.cloned.1.call-done = f32[4,128,2,192]{1,3,0,2:T(8,128)} async-done(((f32[4,512,2,192]{1,3,0,2:T(8,128)}), f32[4,128,2,192]{1,3,0,2:T(8,128)}) %reduce-scatter.13.cloned.1.call-update) | async-done | bytes 786448 | tf_op jit(solution)/shard_map/reduce_scatter | solution.py:206
  1022.9 2.0 convert.53
  1024.9 38.9 %reduce-scatter.19.cloned.1.call-done = f32[4,128,2,192]{1,3,0,2:T(8,128)} async-done(((f32[4,512,2,192]{1,3,0,2:T(8,128)}), f32[4,128,2,192]{1,3,0,2:T(8,128)}) %reduce-scatter.19.cloned.1.call-update) | async-done | bytes 786448 | tf_op jit(solution)/shard_map/reduce_scatter | solution.py:206
  1070.0 2.8 copy.160
  1075.9 2.0 convolution_bitcast_fusion
  1078.0 2.0 convolution_bitcast_fusion.1
  1080.0 2.0 convolution_bitcast_fusion.2
  1082.9 2.0 convolution_bitcast_fusion.3
  1086.3 2.2 fusion.179
  1091.8 2.5 add_add_fusion.1
  1100.9 2.3 add_add_fusion
  1112.1 23.7 %all-reduce.12 = (f32[2,192]{1,0:T(2,128)}, f32[768]{0:T(1024)S(1)}, f32[768]{0:T(1024)S(1)}, f32[768]{0:T(1024)S(1)}, f32[768]{0:T(1024)}, /*index=5*/f32[768]{0:T(1024)S(1)}, f32[768]{0:T(1024)S(1)}, f32[768]{0:T(1024)S(1)}) all-reduce(f32[2,192]{1,0:T(2,128)S(1)} %fusion.133, ...), channel_id=1, replica_groups=mesh['fsdp'=2,'ctx'=4,'tp'=4] {'fsdp','ctx'}, use_global_device_ids=true, to_apply=%region_72.73 | all-reduce | flops 5760 | bytes 46080 | tf_op jit(solution)/shard_map/psum | solution.py:237
  1139.3 6.7 reduce-scatter.25.cloned.1.call-done
  1148.0 223.4 %all-reduce.23.cloned.1.call-done = (f32[512,768]{1,0:T(8,128)}, f32[512,768]{1,0:T(8,128)}, f32[512,768]{1,0:T(8,128)}, f32[512,768]{1,0:T(8,128)}) async-done(((f32[512,768]{1,0:T(8,128)}, f32[512,768]{1,0:T(8,128)}, f32[512,768]{1,0:T(8,128)}, f32[512,768]{1,0:T(8,128)}), (f32[512,768]{1,0:T(8,128)}, f32[512,768]{1,0:T(8,128)}, f32[512,768]{1,0:T(8,128)}, ...) | async-done | bytes 6291472 | tf_op jit(solution)/shard_map/psum | solution.py:12
  1379.7 36.8 %reduce-scatter.21.cloned.1.call-done = f32[96,768]{1,0:T(8,128)} async-done(((f32[768,768]{1,0:T(8,128)}), f32[96,768]{1,0:T(8,128)}) %reduce-scatter.21.cloned.1.call-update) | async-done | bytes 294928 | tf_op jit(solution)/shard_map/reduce_scatter | solution.py:227
  1416.5 46.2 %reduce-scatter.23.cloned.1.call-done = f32[768,96]{0,1:T(8,128)} async-done(((f32[768,768]{0,1:T(8,128)}), f32[768,96]{0,1:T(8,128)}) %reduce-scatter.23.cloned.1.call-update) | async-done | bytes 294928 | tf_op jit(solution)/shard_map/reduce_scatter | solution.py:228
  (727 shorter events, 162.7 us)
Async XLA Ops:
  8.0 47.8 %all-gather.17.cloned.1.call-start = ((), (), s32[]{:S(2)}) async-start(), calls=%async_computation.13 | async-start | bytes 1966080 | tf_op jit(solution)/shard_map/all_gather | solution.py:107
  11.0 18.3 %copy-start.55 = (bf16[4,128,768]{2,1,0:T(8,128)(2,1)}, bf16[4,128,768]{2,1,0:T(8,128)(2,1)S(1)}, u32[]{:S(2)}) copy-start(bf16[4,128,768]{2,1,0:T(8,128)(2,1)S(1)} %get-tuple-element.170) | copy-start | bytes 2359300
  11.0 19.0 %copy-start.56 = (bf16[4,128,768]{2,1,0:T(8,128)(2,1)}, bf16[4,128,768]{2,1,0:T(8,128)(2,1)S(1)}, u32[]{:S(2)}) copy-start(bf16[4,128,768]{2,1,0:T(8,128)(2,1)S(1)} %get-tuple-element.171) | copy-start | bytes 2359300
  11.1 20.7 %copy-start.57 = (bf16[4,128,768]{2,1,0:T(8,128)(2,1)}, bf16[4,128,768]{2,1,0:T(8,128)(2,1)S(1)}, u32[]{:S(2)}) copy-start(bf16[4,128,768]{2,1,0:T(8,128)(2,1)S(1)} %get-tuple-element.172) | copy-start | bytes 2359300
  34.7 42.7 %all-gather.15.cloned.1.call-start = ((), (), s32[]{:S(2)}) async-start(), calls=%async_computation.12 | async-start | bytes 1966080 | tf_op jit(solution)/shard_map/all_gather | solution.py:107
  35.7 63.2 %all-gather.13.cloned.1.call-start = ((), (), s32[]{:S(2)}) async-start(), calls=%async_computation.11 | async-start | bytes 1966080 | tf_op jit(solution)/shard_map/all_gather | solution.py:107
  36.6 83.5 %all-gather.7.cloned.1.call-start = ((), (), s32[]{:S(2)}) async-start(), calls=%async_computation.8 | async-start | bytes 1966080 | tf_op jit(solution)/shard_map/all_gather | solution.py:107
  37.6 11.6 copy-start.202
  37.6 313.7 %all-reduce.29.cloned.1.call-start = ((), (), s32[]{:S(2)}) async-start(), calls=%async_computation.25 | async-start | bytes 12582912 | tf_op jit(solution)/shard_map/psum | solution.py:12
  57.8 24.1 %copy-start.72 = (bf16[4,512,1,192]{1,3,0,2:T(8,128)(2,1)}, bf16[4,512,1,192]{1,3,0,2:T(8,128)(2,1)S(1)}, u32[]{:S(2)}) copy-start(bf16[4,512,1,192]{1,3,0,2:T(8,128)(2,1)S(1)} %copy.123) | copy-start | bytes 2359300
  58.0 21.7 %copy-start.59 = (bf16[4,512,1,192]{1,3,0,2:T(8,128)(2,1)}, bf16[4,512,1,192]{1,3,0,2:T(8,128)(2,1)S(1)}, u32[]{:S(2)}) copy-start(bf16[4,512,1,192]{1,3,0,2:T(8,128)(2,1)S(1)} %copy.124) | copy-start | bytes 2359300
  79.5 6.6 copy-start.75
  79.6 4.7 copy-start.61
  88.2 17.3 %copy-start.89 = (bf16[4,128,3,64]{1,0,3,2:T(4,128)(2,1)}, bf16[4,128,3,64]{1,0,3,2:T(4,128)(2,1)S(1)}, u32[]{:S(2)}) copy-start(bf16[4,128,3,64]{1,0,3,2:T(4,128)(2,1)S(1)} %copy.126) | copy-start | bytes 589828
  88.3 18.7 %copy-start.91 = (bf16[4,128,3,64]{1,0,3,2:T(4,128)(2,1)}, bf16[4,128,3,64]{1,0,3,2:T(4,128)(2,1)S(1)}, u32[]{:S(2)}) copy-start(bf16[4,128,3,64]{1,0,3,2:T(4,128)(2,1)S(1)} %copy.121) | copy-start | bytes 589828
  128.2 232.1 %all-gather.9.cloned.1.call-start = ((), (), s32[]{:S(2)}) async-start(), calls=%async_computation.9 | async-start | bytes 1327104 | tf_op jit(solution)/shard_map/all_gather | solution.py:76
  128.8 245.2 %all-gather.11.cloned.1.call-start = ((), (), s32[]{:S(2)}) async-start(), calls=%async_computation.10 | async-start | bytes 1327104 | tf_op jit(solution)/shard_map/all_gather | solution.py:77
  129.4 488.4 %all-reduce.27.cloned.1.call-start = ((), (), s32[]{:S(2)}) async-start(), calls=%async_computation.24 | async-start | bytes 12582912 | tf_op jit(solution)/shard_map/psum | solution.py:12
  163.1 457.7 %copy-start.130 = (f32[768]{0:T(1024)}, f32[768]{0:T(1024)S(1)}, u32[]{:S(2)}) copy-start(f32[768]{0:T(1024)S(1)} %convert_element_type.382) | copy-start | bytes 9220
  356.2 4.1 copy-start.132
  360.3 7.9 copy-start.10
  360.3 7.9 copy-start.141
  360.3 7.9 copy-start.157
  360.3 7.9 copy-start.211
  360.3 7.9 copy-start.217
  374.0 3.6 copy-start.117
  374.0 3.6 copy-start.220
  395.8 483.1 %all-reduce.25.cloned.1.call-start = ((), (), s32[]{:S(2)}) async-start(), calls=%async_computation.23 | async-start | bytes 12582912 | tf_op jit(solution)/shard_map/psum | solution.py:12
  634.8 12.3 copy-start.50
  634.8 3.9 copy-start.236
  637.9 4.7 copy-start.36
  637.9 13.7 copy-start.52
  657.0 299.4 %reduce-scatter.17.cloned.1.call-start = ((), (), s32[]{:S(2)}) async-start(), calls=%async_computation.16 | async-start | bytes 3932160 | tf_op jit(solution)/shard_map/reduce_scatter | solution.py:206
  878.9 5.6 copy-start.7
  878.9 5.6 copy-start.12
  878.9 5.6 copy-start.22
  878.9 5.6 copy-start.37
  878.9 6.1 copy-start.48
  878.9 6.5 copy-start.104
  878.9 6.9 copy-start.105
  878.9 6.9 copy-start.133
  878.9 6.9 copy-start.143
  879.0 6.9 copy-start.148
  879.0 6.9 copy-start.159
  879.0 6.9 copy-start.163
  885.9 3.8 copy-start.17
  885.9 3.8 copy-start.138
  885.9 3.8 copy-start.155
  905.7 77.1 %reduce-scatter.15.cloned.1.call-start = ((), (), s32[]{:S(2)}) async-start(), calls=%async_computation.15 | async-start | bytes 3932160 | tf_op jit(solution)/shard_map/reduce_scatter | solution.py:206
  910.6 4.0 copy-start.3
  919.5 103.4 %reduce-scatter.13.cloned.1.call-start = ((), (), s32[]{:S(2)}) async-start(), calls=%async_computation.14 | async-start | bytes 3932160 | tf_op jit(solution)/shard_map/reduce_scatter | solution.py:206
  931.6 4.6 copy-start.1
  931.6 132.2 %reduce-scatter.19.cloned.1.call-start = ((), (), s32[]{:S(2)}) async-start(), calls=%async_computation.17 | async-start | bytes 3932160 | tf_op jit(solution)/shard_map/reduce_scatter | solution.py:206
  943.3 164.0 %reduce-scatter.27.cloned.1.call-start = ((), (), s32[]{:S(2)}) async-start(), calls=%async_computation.21 | async-start | bytes 884736
  956.3 189.8 %reduce-scatter.25.cloned.1.call-start = ((), (), s32[]{:S(2)}) async-start(), calls=%async_computation.20 | async-start | bytes 2211840
  1072.8 298.6 %all-reduce.23.cloned.1.call-start = ((), (), s32[]{:S(2)}) async-start(), calls=%async_computation.22 | async-start | bytes 12582912 | tf_op jit(solution)/shard_map/psum | solution.py:12
  1085.0 3.6 copy-start.23
  1085.0 3.6 copy-start.149
  1085.0 3.6 copy-start.164
  1085.0 331.5 %reduce-scatter.21.cloned.1.call-start = ((), (), s32[]{:S(2)}) async-start(), calls=%async_computation.18 | async-start | bytes 2654208 | tf_op jit(solution)/shard_map/reduce_scatter | solution.py:227
  1094.4 368.3 %reduce-scatter.23.cloned.1.call-start = ((), (), s32[]{:S(2)}) async-start(), calls=%async_computation.19 | async-start | bytes 2654208 | tf_op jit(solution)/shard_map/reduce_scatter | solution.py:228
  1106.9 4.7 copy-start.113
  1106.9 4.9 copy-start.115
  1110.2 261.3 %copy-start.33 = (f32[512,768]{1,0:T(8,128)S(1)}, f32[512,768]{1,0:T(8,128)}, u32[]{:S(2)}) copy-start(f32[512,768]{1,0:T(8,128)} %get-tuple-element.214) | copy-start | bytes 4718596
  (191 other events, 343.8 us)
Sparse Core Ops, SparseCore 0:
  34.8 20.9 all-gather.16
  57.3 20.0 all-gather.14
  79.0 19.8 all-gather.12
  100.3 19.8 all-gather.6
  128.3 222.9 all-reduce.28
  396.0 221.7 all-reduce.26
  657.1 221.7 all-reduce.24
  905.8 36.6 reduce-scatter.16
  945.0 37.7 reduce-scatter.14
  985.2 37.7 reduce-scatter.12
  1026.0 37.7 reduce-scatter.18
  1066.8 34.9 reduce-scatter.26
  1105.7 40.3 reduce-scatter.24
  1148.5 222.8 all-reduce.22
  1375.2 41.2 reduce-scatter.20
  1420.3 42.3 reduce-scatter.22
Sparse Core Ops, SparseCore 1:
  130.6 24.0 all-gather.8
  156.4 23.8 all-gather.10
where the time goes:
time: 1480 us; the launch traced here: 1470 us
  waiting for transfers between devices  1080 us (73%)
  matrix products  123 us (8%)
  local copies, waits for them, and re-layouts  88.7 us (6%)
  other arithmetic  83.5 us (6%)
  blocking collectives  74.4 us (5%)
  between operations  20 us (1%)
    psum x4, waiting for transfers between devices, tp_total(): return lax.psum(partial_sum, 'tp')  845 us
    reduce_scatter x4, waiting for transfers between devices, on_device(): lax.psum_scatter(key_value_terms, 'ctx', scatter_dimension=1, tiled=True)  99.3 us
    unnamed x504, local copies, waits for them, and re-layouts  59.3 us
    reduce_scatter x1, waiting for transfers between devices, on_device(): lax.psum_scatter(grad_wdown, ('fsdp', 'ctx'), scatter_dimension=1, tiled=...  46.2 us
    all_gather x4, waiting for transfers between devices, on_device(): key_value = lax.all_gather(kv_local, 'ctx', axis=1, tiled=True)  44 us
    reduce_scatter x1, waiting for transfers between devices, on_device(): lax.psum_scatter(grad_win, ('fsdp', 'ctx'), scatter_dimension=0, tiled=True)  36.8 us
  transfers between devices with their start and end apart: 18, of which 14 were waited for; matrix products, arithmetic and copies ran while one was open for 11% of the time, Pallas kernels for 0%

commit v1 on v0

--- a/solution.py
+++ b/solution.py
@@ -6,6 +6,18 @@
 HD = 64
 SLOT_MB = 4
 epsilon = 1e-05
+
+
+def doubled_up(shard, axis, dim):
+    ways, here = (lax.axis_size(axis), lax.axis_index(axis))
+    grown, reach = (shard, 1)
+    while reach < ways:
+        theirs = lax.ppermute(grown, axis, [(d, d ^ reach) for d in range(ways)])
+        mine_first = jnp.concatenate([grown, theirs], axis=dim)
+        theirs_first = jnp.concatenate([theirs, grown], axis=dim)
+        grown = jnp.where(here & reach == 0, mine_first, theirs_first)
+        reach = 2 * reach
+    return grown
 
 
 def tp_total(partial_sum):
@@ -104,7 +116,7 @@
             + bias_three
         ).astype(jnp.bfloat16)
         kv_local = qkv_local[:, 1:].reshape(slot_batch, row_count, 2, local_width)
-        key_value = lax.all_gather(kv_local, "ctx", axis=1, tiled=True)
+        key_value = doubled_up(kv_local, "ctx", 1)
         queries = qkv_local[:, 0].reshape(slot_batch, row_count, head_count, HD)
         keys_all = key_value[:, :, 0].reshape(slot_batch, key_count, head_count, HD)
         values_all = key_value[:, :, 1].reshape(slot_batch, key_count, head_count, HD)

time: 1480 us -> 1330 us (0.90)
  waiting for transfers between devices: 1080 us -> 900 us
  blocking collectives: 74.4 us -> 93.5 us
  other arithmetic: 83.5 us -> 98.5 us
    psum x4, waiting for transfers between devices: 845 us -> 774 us  [tp_total(): return lax.psum(partial_sum, 'tp')]
    reduce_scatter x1, waiting for transfers between devices: 46.2 us -> 0.01 us  [on_device(): lax.psum_scatter(grad_wdown, ('fsdp', 'ctx'), scatter_dimension=1, tiled=...]
    all_gather x4 -> x0, waiting for transfers between devices: 44 us -> none  [on_device(): key_value = lax.all_gather(kv_local, 'ctx', axis=1, tiled=True)]
    reduce_scatter x1, waiting for transfers between devices: 36.8 us -> 0.01 us  [on_device(): lax.psum_scatter(grad_win, ('fsdp', 'ctx'), scatter_dimension=0, tiled=True)]
    ppermute x0 -> x8, waiting for transfers between devices: none -> 20.4 us  [doubled_up(): theirs = lax.ppermute(grown, axis, [(d, d ^ reach) for d in range(ways)])]
    unnamed x504 -> x508, local copies, waits for them, and re-layouts: 59.3 us -> 59.4 us
  transfers between devices with their start and end apart: 18 -> 22, of which waited for: 14 -> 11; matrix products, arithmetic and copies ran while one was open for 11% -> 13% of each run, Pallas kernels for 0% -> 0%
where the time goes in v1:
time: 1330 us; the launch traced here: 1320 us
  waiting for transfers between devices  900 us (68%)
  matrix products  123 us (9%)
  other arithmetic  98.5 us (7%)
  blocking collectives  93.5 us (7%)
  local copies, waits for them, and re-layouts  80 us (6%)
  between operations  20.1 us (2%)
    psum x4, waiting for transfers between devices, tp_total(): return lax.psum(partial_sum, 'tp')  774 us
    reduce_scatter x4, waiting for transfers between devices, on_device(): lax.psum_scatter(key_value_terms, 'ctx', scatter_dimension=1, tiled=True)  99.2 us
    unnamed x508, local copies, waits for them, and re-layouts  59.4 us
    unnamed x1, blocking collectives  33.1 us
  transfers between devices with their start and end apart: 22, of which 11 were waited for; matrix products, arithmetic and copies ran while one was open for 13% of the time, Pallas kernels for 0%

profile of v1, /device:TPU:0, one launch (start us, length us, event | category | flops | bytes accessed | tf_op | source)
XLA Modules:
  0.0 1321.5 jit_solution(7072063190319602990)
XLA Ops:
  8.1 3.0 fusion.200
  11.2 15.5 %all_gather.20 = bf16[768,3,192]{2,1,0:T(4,128)(2,1)} all-gather(bf16[96,3,192]{2,1,0:T(4,128)(2,1)S(1)} %copy.105), channel_id=1, replica_groups=mesh['fsdp'=2,'ctx'=4,'tp'=4] {'fsdp','ctx'}, dimensions={0}, use_global_device_ids=true | all-gather | bytes 995328 | tf_op jit(solution)/shard_map/all_gather | solution.py:86
  26.7 2.6 copy.106
  42.0 20.1 %all_gather.21 = bf16[192,768]{0,1:T(8,128)(2,1)S(1)} all-gather(bf16[192,96]{0,1:T(8,128)(2,1)S(1)} %copy.111), channel_id=1, replica_groups=mesh['fsdp'=2,'ctx'=4,'tp'=4] {'fsdp','ctx'}, dimensions={1}, use_global_device_ids=true | all-gather | bytes 331776 | tf_op jit(solution)/shard_map/all_gather | solution.py:87
  65.3 2.2 maximum_select_fusion.5
  68.3 2.2 maximum_select_fusion.4
  72.0 2.9 maximum_select_fusion.3
  79.9 4.5 collective-permute-done.5
  90.5 10.6 collective-permute-done.3
  112.1 5.3 collective-permute-done.1
  133.5 33.1 %all-reduce.17 = (bf16[768]{0:T(1024)(128)(2,1)}, bf16[768]{0:T(1024)(128)(2,1)}, bf16[768]{0:T(1024)(128)(2,1)}, bf16[768]{0:T(1024)(128)(2,1)}, bf16[768]{0:T(1024)(128)(2,1)}, /*index=5*/bf16[768]{0:T(1024)(128)(2,1)}) all-reduce(bf16[768]{0:T(1024)(128)(2,1)S(1)} %dynamic-update-slice, ...), channel_id=1, replica_groups=mesh['fsdp'=2,'ctx'=4,'tp'=4] {'fsdp','ctx'}, use_global_device_ids=true, to_apply=%add | all-reduce | flops 4608 | bytes 18432
  168.6 180.3 %all-reduce.29.cloned.1.call-done = (f32[512,768]{1,0:T(8,128)}, f32[512,768]{1,0:T(8,128)}, f32[512,768]{1,0:T(8,128)}, f32[512,768]{1,0:T(8,128)}) async-done(((f32[512,768]{1,0:T(8,128)}, f32[512,768]{1,0:T(8,128)}, f32[512,768]{1,0:T(8,128)}, f32[512,768]{1,0:T(8,128)}), (f32[512,768]{1,0:T(8,128)}, f32[512,768]{1,0:T(8,128)}, f32[512,768]{1,0:T(8,128)}, ...) | async-done | bytes 6291472 | tf_op jit(solution)/shard_map/psum | solution.py:24
  348.8 4.6 fusion.193
  358.2 7.8 multiply_convert_fusion.4
  366.1 5.7 multiply_convert_fusion.5
  371.7 3.6 fusion.223
  375.4 2.0 fusion.221
  377.4 5.5 multiply_convert_fusion.6
  382.9 2.0 fusion.219
  384.9 5.8 multiply_convert_fusion.7
  391.7 2.0 fusion.217
  398.2 3.8 multiply_reduce_fusion.23
  403.2 212.4 %all-reduce.27.cloned.1.call-done = (f32[512,768]{1,0:T(8,128)}, f32[512,768]{1,0:T(8,128)}, f32[512,768]{1,0:T(8,128)}, f32[512,768]{1,0:T(8,128)}) async-done(((f32[512,768]{1,0:T(8,128)}, f32[512,768]{1,0:T(8,128)}, f32[512,768]{1,0:T(8,128)}, f32[512,768]{1,0:T(8,128)}), (f32[512,768]{1,0:T(8,128)}, f32[512,768]{1,0:T(8,128)}, f32[512,768]{1,0:T(8,128)}, ...) | async-done | bytes 6291472 | tf_op jit(solution)/shard_map/psum | solution.py:24
  615.6 2.6 fusion.191
  619.9 3.1 fusion.188
  624.9 2.7 multiply_reduce_fusion.4
  629.5 3.1 convert_reduce_fusion.2
  632.7 3.1 convert_reduce_fusion.3
  638.4 2.1 fusion.227
  642.9 2.0 fusion.226
  647.4 2.0 fusion.225
  652.8 2.0 fusion.224
  655.6 221.2 %all-reduce.25.cloned.1.call-done = (f32[512,768]{1,0:T(8,128)}, f32[512,768]{1,0:T(8,128)}, f32[512,768]{1,0:T(8,128)}, f32[512,768]{1,0:T(8,128)}) async-done(((f32[512,768]{1,0:T(8,128)}, f32[512,768]{1,0:T(8,128)}, f32[512,768]{1,0:T(8,128)}, f32[512,768]{1,0:T(8,128)}), (f32[512,768]{1,0:T(8,128)}, f32[512,768]{1,0:T(8,128)}, f32[512,768]{1,0:T(8,128)}, ...) | async-done | bytes 6291472 | tf_op jit(solution)/shard_map/psum | solution.py:24
  876.9 5.5 multiply_reduce_fusion.11
  883.8 3.8 convert_reduce_fusion.11
  887.7 3.8 convert_reduce_fusion.10
  895.4 3.4 multiply_reduce_fusion.1
  901.6 2.0 pad_maximum_fusion.3
  904.3 2.5 convolution_convert_fusion.2
  908.5 4.1 multiply_reduce_fusion.2
  915.5 1.9 pad_maximum_fusion.2
  918.2 2.5 convolution_convert_fusion.3
  922.4 2.3 multiply_reduce_fusion.3
  927.5 1.9 pad_maximum_fusion.1
  930.6 2.5 convolution_convert_fusion
  934.1 2.2 multiply_reduce_fusion
  939.1 2.0 pad_maximum_fusion.4
  955.5 2.8 fusion.73
  958.2 22.1 %reduce-scatter.15.cloned.1.call-done = f32[4,128,2,192]{1,3,0,2:T(8,128)} async-done(((f32[4,512,2,192]{1,3,0,2:T(8,128)}), f32[4,128,2,192]{1,3,0,2:T(8,128)}) %reduce-scatter.15.cloned.1.call-update) | async-done | bytes 786448 | tf_op jit(solution)/shard_map/reduce_scatter | solution.py:218
  980.4 2.0 convert.55
  982.3 38.3 %reduce-scatter.13.cloned.1.call-done = f32[4,128,2,192]{1,3,0,2:T(8,128)} async-done(((f32[4,512,2,192]{1,3,0,2:T(8,128)}), f32[4,128,2,192]{1,3,0,2:T(8,128)}) %reduce-scatter.13.cloned.1.call-update) | async-done | bytes 786448 | tf_op jit(solution)/shard_map/reduce_scatter | solution.py:218
  1020.6 2.0 convert.53
  1022.6 38.8 %reduce-scatter.19.cloned.1.call-done = f32[4,128,2,192]{1,3,0,2:T(8,128)} async-done(((f32[4,512,2,192]{1,3,0,2:T(8,128)}), f32[4,128,2,192]{1,3,0,2:T(8,128)}) %reduce-scatter.19.cloned.1.call-update) | async-done | bytes 786448 | tf_op jit(solution)/shard_map/reduce_scatter | solution.py:218
  1067.6 2.8 copy.160
  1073.6 2.0 convolution_bitcast_fusion
  1075.6 2.0 convolution_bitcast_fusion.1
  1077.7 2.0 convolution_bitcast_fusion.2
  1080.6 2.0 convolution_bitcast_fusion.3
  1084.0 2.2 fusion.179
  1090.2 2.5 add_add_fusion.1
  1099.2 2.4 add_add_fusion
  1110.4 24.8 %all-reduce.12 = (f32[2,192]{1,0:T(2,128)}, f32[768]{0:T(1024)S(1)}, f32[768]{0:T(1024)S(1)}, f32[768]{0:T(1024)S(1)}, f32[768]{0:T(1024)}, /*index=5*/f32[768]{0:T(1024)S(1)}, f32[768]{0:T(1024)S(1)}, f32[768]{0:T(1024)S(1)}) all-reduce(f32[2,192]{1,0:T(2,128)S(1)} %fusion.133, ...), channel_id=1, replica_groups=mesh['fsdp'=2,'ctx'=4,'tp'=4] {'fsdp','ctx'}, use_global_device_ids=true, to_apply=%region_72.73 | all-reduce | flops 5760 | bytes 46080 | tf_op jit(solution)/shard_map/psum | solution.py:249
  1138.7 4.7 reduce-scatter.25.cloned.1.call-done
  1145.4 160.2 %all-reduce.23.cloned.1.call-done = (f32[512,768]{1,0:T(8,128)}, f32[512,768]{1,0:T(8,128)}, f32[512,768]{1,0:T(8,128)}, f32[512,768]{1,0:T(8,128)}) async-done(((f32[512,768]{1,0:T(8,128)}, f32[512,768]{1,0:T(8,128)}, f32[512,768]{1,0:T(8,128)}, f32[512,768]{1,0:T(8,128)}), (f32[512,768]{1,0:T(8,128)}, f32[512,768]{1,0:T(8,128)}, f32[512,768]{1,0:T(8,128)}, ...) | async-done | bytes 6291472 | tf_op jit(solution)/shard_map/psum | solution.py:24
  (743 shorter events, 166.5 us)
Async XLA Ops:
  8.0 340.8 %all-reduce.29.cloned.1.call-start = ((), (), s32[]{:S(2)}) async-start(), calls=%async_computation.21 | async-start | bytes 12582912 | tf_op jit(solution)/shard_map/psum | solution.py:24
  11.0 18.3 %copy-start.55 = (bf16[4,128,768]{2,1,0:T(8,128)(2,1)}, bf16[4,128,768]{2,1,0:T(8,128)(2,1)S(1)}, u32[]{:S(2)}) copy-start(bf16[4,128,768]{2,1,0:T(8,128)(2,1)S(1)} %get-tuple-element.170) | copy-start | bytes 2359300
  11.0 19.0 %copy-start.56 = (bf16[4,128,768]{2,1,0:T(8,128)(2,1)}, bf16[4,128,768]{2,1,0:T(8,128)(2,1)S(1)}, u32[]{:S(2)}) copy-start(bf16[4,128,768]{2,1,0:T(8,128)(2,1)S(1)} %get-tuple-element.171) | copy-start | bytes 2359300
  11.1 20.7 %copy-start.57 = (bf16[4,128,768]{2,1,0:T(8,128)(2,1)}, bf16[4,128,768]{2,1,0:T(8,128)(2,1)S(1)}, u32[]{:S(2)}) copy-start(bf16[4,128,768]{2,1,0:T(8,128)(2,1)S(1)} %get-tuple-element.172) | copy-start | bytes 2359300
  33.9 2.5 collective-permute-start.6
  34.5 27.6 %collective-permute-start.4 = (bf16[4,128,2,192]{1,0,3,2:T(4,128)(2,1)S(1)}, bf16[4,128,2,192]{1,0,3,2:T(4,128)(2,1)}, u32[]{:S(2)}, u32[]{:S(2)}) collective-permute-start(bf16[4,128,2,192]{1,0,3,2:T(4,128)(2,1)S(1)} %reshape.611), channel_id=1, source_target_pairs={{0,4},{4,0},{8,12},{12,8},{1,5},{5,1},{9,13},{13,9},{2,6},{6,2},{1... | collective-permute-start | bytes 1179656 | tf_op jit(solution)/shard_map/ppermute | solution.py:15
  34.9 30.5 %collective-permute-start.2 = (bf16[4,128,2,192]{1,0,3,2:T(4,128)(2,1)S(1)}, bf16[4,128,2,192]{1,0,3,2:T(4,128)(2,1)}, u32[]{:S(2)}, u32[]{:S(2)}) collective-permute-start(bf16[4,128,2,192]{1,0,3,2:T(4,128)(2,1)S(1)} %reshape.607), channel_id=1, source_target_pairs={{0,4},{4,0},{8,12},{12,8},{1,5},{5,1},{9,13},{13,9},{2,6},{6,2},{1... | collective-permute-start | bytes 1179656 | tf_op jit(solution)/shard_map/ppermute | solution.py:15
  36.2 32.1 %collective-permute-start = (bf16[4,128,2,192]{1,0,3,2:T(4,128)(2,1)}, bf16[4,128,2,192]{1,0,3,2:T(4,128)(2,1)}, u32[]{:S(2)}, u32[]{:S(2)}) collective-permute-start(bf16[4,128,2,192]{1,0,3,2:T(4,128)(2,1)} %reshape.603), channel_id=1, source_target_pairs={{0,4},{4,0},{8,12},{12,8},{1,5},{5,1},{9,13},{13,9},{2,6},{6,2},{1... | collective-permute-start | bytes 1179656 | tf_op jit(solution)/shard_map/ppermute | solution.py:15
  36.4 4.5 copy-start.205
  36.4 4.5 copy-start.206
  36.4 4.5 copy-start.207
  36.4 4.6 copy-start.208
  36.4 4.6 copy-start.152
  38.2 33.8 %collective-permute-start.7 = (bf16[4,256,2,192]{1,0,3,2:T(4,128)(2,1)S(1)}, bf16[4,256,2,192]{1,0,3,2:T(4,128)(2,1)}, u32[]{:S(2)}, u32[]{:S(2)}) collective-permute-start(bf16[4,256,2,192]{1,0,3,2:T(4,128)(2,1)S(1)} %maximum_select_fusion.7), channel_id=1, source_target_pairs={{0,8},{4,12},{8,0},{12,4},{1,9},{5,13},{9,1},{13,5},{2,10},{6,14},... | collective-permute-start | bytes 2359304 | tf_op jit(solution)/shard_map/ppermute | solution.py:15
  41.2 34.6 %copy-start.82 = (bf16[4,128,3,64]{1,0,3,2:T(4,128)(2,1)}, bf16[4,128,3,64]{1,0,3,2:T(4,128)(2,1)S(1)}, u32[]{:S(2)}) copy-start(bf16[4,128,3,64]{1,0,3,2:T(4,128)(2,1)S(1)} %reshape_squeeze.46) | copy-start | bytes 589828
  41.2 45.2 %copy-start.88 = (bf16[4,128,3,64]{1,0,3,2:T(4,128)(2,1)}, bf16[4,128,3,64]{1,0,3,2:T(4,128)(2,1)S(1)}, u32[]{:S(2)}) copy-start(bf16[4,128,3,64]{1,0,3,2:T(4,128)(2,1)S(1)} %reshape_squeeze.43) | copy-start | bytes 589828
  41.3 62.0 %copy-start.86 = (bf16[4,128,3,64]{1,0,3,2:T(4,128)(2,1)}, bf16[4,128,3,64]{1,0,3,2:T(4,128)(2,1)S(1)}, u32[]{:S(2)}) copy-start(bf16[4,128,3,64]{1,0,3,2:T(4,128)(2,1)S(1)} %reshape_squeeze.40) | copy-start | bytes 589828
  63.8 20.5 %collective-permute-start.5 = (bf16[4,256,2,192]{1,0,3,2:T(4,128)(2,1)S(1)}, bf16[4,256,2,192]{1,0,3,2:T(4,128)(2,1)S(1)}, u32[]{:S(2)}, u32[]{:S(2)}) collective-permute-start(bf16[4,256,2,192]{1,0,3,2:T(4,128)(2,1)S(1)} %maximum_select_fusion.6), channel_id=1, source_target_pairs={{0,8},{4,12},{8,0},{12,4},{1,9},{5,13},{9,1},{13,5},{2,10},{6,14},... | collective-permute-start | bytes 2359304 | tf_op jit(solution)/shard_map/ppermute | solution.py:15
  67.6 33.6 %collective-permute-start.3 = (bf16[4,256,2,192]{1,0,3,2:T(4,128)(2,1)S(1)}, bf16[4,256,2,192]{1,0,3,2:T(4,128)(2,1)S(1)}, u32[]{:S(2)}, u32[]{:S(2)}) collective-permute-start(bf16[4,256,2,192]{1,0,3,2:T(4,128)(2,1)S(1)} %maximum_select_fusion.5), channel_id=1, source_target_pairs={{0,8},{4,12},{8,0},{12,4},{1,9},{5,13},{9,1},{13,5},{2,10},{6,14},... | collective-permute-start | bytes 2359304 | tf_op jit(solution)/shard_map/ppermute | solution.py:15
  70.5 46.9 %collective-permute-start.1 = (bf16[4,256,2,192]{1,0,3,2:T(4,128)(2,1)S(1)}, bf16[4,256,2,192]{1,0,3,2:T(4,128)(2,1)S(1)}, u32[]{:S(2)}, u32[]{:S(2)}) collective-permute-start(bf16[4,256,2,192]{1,0,3,2:T(4,128)(2,1)S(1)} %maximum_select_fusion.4), channel_id=1, source_target_pairs={{0,8},{4,12},{8,0},{12,4},{1,9},{5,13},{9,1},{13,5},{2,10},{6,14},... | collective-permute-start | bytes 2359304 | tf_op jit(solution)/shard_map/ppermute | solution.py:15
  79.8 27.5 %copy-start.90 = (bf16[4,128,3,64]{1,0,3,2:T(4,128)(2,1)}, bf16[4,128,3,64]{1,0,3,2:T(4,128)(2,1)S(1)}, u32[]{:S(2)}) copy-start(bf16[4,128,3,64]{1,0,3,2:T(4,128)(2,1)S(1)} %copy.126) | copy-start | bytes 589828
  90.5 18.4 %copy-start.92 = (bf16[4,128,3,64]{1,0,3,2:T(4,128)(2,1)}, bf16[4,128,3,64]{1,0,3,2:T(4,128)(2,1)S(1)}, u32[]{:S(2)}) copy-start(bf16[4,128,3,64]{1,0,3,2:T(4,128)(2,1)S(1)} %copy.121) | copy-start | bytes 589828
  125.5 232.7 %all-gather.3.cloned.1.call-start = ((), (), s32[]{:S(2)}) async-start(), calls=%async_computation.8 | async-start | bytes 1327104 | tf_op jit(solution)/shard_map/all_gather | solution.py:88
  126.1 245.7 %all-gather.5.cloned.1.call-start = ((), (), s32[]{:S(2)}) async-start(), calls=%async_computation.9 | async-start | bytes 1327104 | tf_op jit(solution)/shard_map/all_gather | solution.py:89
  126.7 489.0 %all-reduce.27.cloned.1.call-start = ((), (), s32[]{:S(2)}) async-start(), calls=%async_computation.20 | async-start | bytes 12582912 | tf_op jit(solution)/shard_map/psum | solution.py:24
  167.9 450.7 %copy-start.132 = (f32[768]{0:T(1024)}, f32[768]{0:T(1024)S(1)}, u32[]{:S(2)}) copy-start(f32[768]{0:T(1024)S(1)} %convert_element_type.382) | copy-start | bytes 9220
  353.8 4.4 copy-start.134
  358.2 7.9 copy-start.10
  358.2 7.9 copy-start.143
  358.2 7.9 copy-start.159
  358.2 7.9 copy-start.213
  358.2 7.9 copy-start.219
  393.7 483.1 %all-reduce.25.cloned.1.call-start = ((), (), s32[]{:S(2)}) async-start(), calls=%async_computation.19 | async-start | bytes 12582912 | tf_op jit(solution)/shard_map/psum | solution.py:24
  632.6 12.3 copy-start.50
  632.7 3.9 copy-start.238
  635.7 4.7 copy-start.36
  635.7 13.7 %copy-start.52 = (f32[512,768]{1,0:T(8,128)}, f32[512,768]{1,0:T(8,128)S(1)}, u32[]{:S(2)}) copy-start(f32[512,768]{1,0:T(8,128)S(1)} %get-tuple-element.125) | copy-start | bytes 4718596
  654.9 299.2 %reduce-scatter.17.cloned.1.call-start = ((), (), s32[]{:S(2)}) async-start(), calls=%async_computation.12 | async-start | bytes 3932160 | tf_op jit(solution)/shard_map/reduce_scatter | solution.py:218
  876.8 5.6 copy-start.7
  876.8 5.6 copy-start.12
  876.8 5.6 copy-start.22
  876.8 5.6 copy-start.37
  876.8 6.1 copy-start.48
  876.8 6.5 copy-start.105
  876.8 6.9 copy-start.106
  876.8 6.9 copy-start.135
  876.8 6.9 copy-start.145
  876.9 6.9 copy-start.150
  876.9 6.9 copy-start.161
  876.9 6.9 copy-start.165
  883.8 3.8 copy-start.17
  903.6 76.8 %reduce-scatter.15.cloned.1.call-start = ((), (), s32[]{:S(2)}) async-start(), calls=%async_computation.11 | async-start | bytes 3932160 | tf_op jit(solution)/shard_map/reduce_scatter | solution.py:218
  908.5 4.1 copy-start.3
  917.5 103.1 %reduce-scatter.13.cloned.1.call-start = ((), (), s32[]{:S(2)}) async-start(), calls=%async_computation.10 | async-start | bytes 3932160 | tf_op jit(solution)/shard_map/reduce_scatter | solution.py:218
  929.4 4.7 copy-start.1
  929.5 131.9 %reduce-scatter.19.cloned.1.call-start = ((), (), s32[]{:S(2)}) async-start(), calls=%async_computation.13 | async-start | bytes 3932160 | tf_op jit(solution)/shard_map/reduce_scatter | solution.py:218
  941.1 164.5 %reduce-scatter.27.cloned.1.call-start = ((), (), s32[]{:S(2)}) async-start(), calls=%async_computation.17 | async-start | bytes 884736
  954.0 189.5 %reduce-scatter.25.cloned.1.call-start = ((), (), s32[]{:S(2)}) async-start(), calls=%async_computation.16 | async-start | bytes 2211840
  1070.5 235.2 %all-reduce.23.cloned.1.call-start = ((), (), s32[]{:S(2)}) async-start(), calls=%async_computation.18 | async-start | bytes 12582912 | tf_op jit(solution)/shard_map/psum | solution.py:24
  1082.6 231.2 %reduce-scatter.21.cloned.1.call-start = ((), (), s32[]{:S(2)}) async-start(), calls=%async_computation.14 | async-start | bytes 2654208 | tf_op jit(solution)/shard_map/reduce_scatter | solution.py:239
  1092.7 221.1 %reduce-scatter.23.cloned.1.call-start = ((), (), s32[]{:S(2)}) async-start(), calls=%async_computation.15 | async-start | bytes 2654208 | tf_op jit(solution)/shard_map/reduce_scatter | solution.py:240
  1105.3 4.7 copy-start.115
  1105.3 4.8 copy-start.117
  1108.6 197.1 %copy-start.33 = (f32[512,768]{1,0:T(8,128)S(1)}, f32[512,768]{1,0:T(8,128)}, u32[]{:S(2)}) copy-start(f32[512,768]{1,0:T(8,128)} %get-tuple-element.214) | copy-start | bytes 4718596
  (197 other events, 366.5 us)
Sparse Core Ops, SparseCore 0:
  125.6 223.1 all-reduce.28
  393.8 221.7 all-reduce.26
  655.0 221.7 all-reduce.24
  1082.7 222.8 all-reduce.22
Sparse Core Ops, SparseCore 1:
  127.9 24.2 all-gather.2
  153.8 23.9 all-gather.4
  903.6 36.5 reduce-scatter.16
  942.8 37.5 reduce-scatter.14
  982.9 37.6 reduce-scatter.12
  1023.7 37.6 reduce-scatter.18
  1064.4 34.9 reduce-scatter.26
  1103.2 40.2 reduce-scatter.24
  1147.3 42.2 reduce-scatter.20
  1193.4 42.2 reduce-scatter.22
